TPU v7x, 8 devices: a whole 2x2x1 slice. The times are simulated.
8 devices in a mesh: batch: 1 (over z), seq_hi: 2 (over y), seq: 4 (over x, core).
Axes of the slice: x: 2, y: 2, z: 1, core: 2. Of those that a mesh axis runs over, the one named last changes fastest.
Arguments:
- x_seq: bfloat16 [24, 1536, 128], P('batch', ('seq_hi', 'seq'))
- w_f0: bfloat16 [2, 10, 128, 128], replicated
- w_f1: bfloat16 [2, 10, 128, 128], replicated
- w_g0: bfloat16 [2, 10, 128, 128], replicated
- w_g1: bfloat16 [2, 10, 128, 128], replicated
- w_res: bfloat16 [2, 10, 128, 128], replicated
- w_skip: bfloat16 [2, 10, 128, 128], replicated
Outputs:
- output 1: float32 [24, 1536, 128], P('batch', ('seq_hi', 'seq'))
- output 2: float32 [24, 1536, 128], P('batch', ('seq_hi', 'seq'))
All inputs are finite; a program needn't handle non-finite values.
Results may differ from a plain program's by a relative error of at most 0.00640755.
Values are sent between devices in bfloat16 or wider.
A program may use at most 1 GiB of HBM per device.

v0:
```python
import functools

import jax
import jax.numpy as jnp
from jax import lax
from jax.experimental import pallas as pl
from jax.experimental.pallas import tpu as pltpu
from jax.sharding import PartitionSpec as P

MESH = pl.DeviceIdType.MESH
SEQ_AXES = ("seq_hi", "seq")
N_DEV = 8
PIECES = 4
LAG = 2
F32 = jnp.float32
BF16 = jnp.bfloat16

PLAN = (
    (
        ((8, 4, (0, 1, 2, 3)), (9, 4, (0, 1, 2, 3)),),
        ((10, 4, (0, 1, 2, 3)), (11, 4, (0, 1, 2, 3)),),
        ((0, 2, (0, 1)), (1, 2, (0, 1)), (2, 2, (0, 1)), (3, 2, (0, 1)),),
        ((4, 2, (0, 1)), (5, 2, (0, 1)), (6, 2, (0, 1)), (7, 2, (0, 1)),),
    ),
    (
        ((12, 4, (0, 1, 2, 3)), (13, 4, (0, 1, 2, 3)),),
        ((14, 4, (0, 1, 2, 3)), (15, 4, (0, 1, 2, 3)),),
        ((16, 2, (0, 1)), (17, 2, (0, 1)), (18, 2, (0, 1)), (19, 2, (0, 1)),),
        ((20, 2, (0, 1)), (21, 2, (0, 1)), (22, 2, (0, 1)), (23, 2, (0, 1)),),
    ),
    (
        ((0, 8, (2, 3, 4, 5, 6, 7)),),
        ((1, 8, (2, 3, 4, 5, 6, 7)),),
        ((2, 8, (2, 3, 4, 5, 6, 7)),),
        ((3, 8, (2, 3, 4, 5, 6, 7)),),
    ),
    (
        ((4, 8, (2, 3, 4, 5, 6, 7)),),
        ((5, 8, (2, 3, 4, 5, 6, 7)),),
        ((6, 8, (2, 3, 4, 5, 6, 7)),),
        ((7, 8, (2, 3, 4, 5, 6, 7)),),
    ),
    (
        ((8, 8, (4, 5, 6, 7)),),
        ((9, 8, (4, 5, 6, 7)),),
        ((10, 8, (4, 5, 6, 7)),),
        ((11, 8, (4, 5, 6, 7)),),
    ),
    (
        ((12, 8, (4, 5, 6, 7)),),
        ((13, 8, (4, 5, 6, 7)),),
        ((14, 8, (4, 5, 6, 7)),),
        ((15, 8, (4, 5, 6, 7)),),
    ),
    (
        ((16, 8, (2, 3, 4, 5, 6, 7)),),
        ((17, 8, (2, 3, 4, 5, 6, 7)),),
        ((18, 8, (2, 3, 4, 5, 6, 7)),),
        ((19, 8, (2, 3, 4, 5, 6, 7)),),
    ),
    (
        ((20, 8, (2, 3, 4, 5, 6, 7)),),
        ((21, 8, (2, 3, 4, 5, 6, 7)),),
        ((22, 8, (2, 3, 4, 5, 6, 7)),),
        ((23, 8, (2, 3, 4, 5, 6, 7)),),
    ),
)
N_SWEEP = max(len(sweeps) for sweeps in PLAN)
KINDS = tuple(sorted({tuple(n for _, n, _ in sweep) for sweeps in PLAN for sweep in sweeps}, reverse=True))


def units(sweep):
    return [(k, *rest) for k, rest in enumerate((seq, b, b in keep) for seq, n, keep in sweep for b in range(n))]


def kernel(n_layers, n_cyc, blk, pad, x_ref, wf0, wf1, wg0, wg1, wr, ws, h_out, s_out,
           x_own, xbuf, wg_v, wo_v, hout_v, skip_v, w_sem, own_sem, x_send, x_recv, o_send, h_recv, s_recv, *state):
    me = lax.axis_index("seq_hi") * 4 + lax.axis_index("seq")
    chan = x_ref.shape[-1]
    n_seq = x_ref.shape[0]
    bufs_of = {kind: state[2 * i:2 * i + 2] for i, kind in enumerate(KINDS)}

    def dev(index):
        return {"seq_hi": index // 4, "seq": index % 4}

    def on(index):
        return pl.when(me == index)

    own = pltpu.make_async_copy(x_ref, x_own, own_sem)
    own.start()
    w_copies = [
        pltpu.make_async_copy(wf1, wg_v.at[:, pl.ds(0, chan), pl.ds(0, chan)], w_sem.at[0]),
        pltpu.make_async_copy(wg1, wg_v.at[:, pl.ds(0, chan), pl.ds(chan, chan)], w_sem.at[1]),
        pltpu.make_async_copy(wf0, wg_v.at[:, pl.ds(chan, chan), pl.ds(0, chan)], w_sem.at[2]),
        pltpu.make_async_copy(wg0, wg_v.at[:, pl.ds(chan, chan), pl.ds(chan, chan)], w_sem.at[3]),
        pltpu.make_async_copy(wr, wo_v.at[:, :, pl.ds(0, chan)], w_sem.at[4]),
        pltpu.make_async_copy(ws, wo_v.at[:, :, pl.ds(chan, chan)], w_sem.at[5]),
    ]
    for copy in w_copies:
        copy.start()

    barrier = pltpu.get_barrier_semaphore()
    for step in range(1, N_DEV):
        other = lax.rem(me + step, N_DEV)
        pl.semaphore_signal(barrier, inc=1, device_id={"seq_hi": other // 4, "seq": lax.rem(other, 4)}, device_id_type=MESH)
    pl.semaphore_wait(barrier, N_DEV - 1)
    own.wait()

    wanted = [[] for _ in range(N_DEV)]
    for target, sweeps in enumerate(PLAN):
        for q, sweep in enumerate(sweeps):
            for k, seq, b, _ in units(sweep):
                wanted[b].append((q, (target // 2) ^ (b // 2) != 3, target, k, seq))
    for src in range(N_DEV):
        @on(src)
        def _():
            for q, _, target, k, seq in sorted(wanted[src]):
                if target == src:
                    pltpu.make_async_copy(x_ref.at[seq], xbuf.at[q, k], x_recv.at[q]).start()
                else:
                    pltpu.make_async_remote_copy(
                        src_ref=x_own.at[seq], dst_ref=xbuf.at[q, k], send_sem=x_send, recv_sem=x_recv.at[q],
                        device_id=dev(target), device_id_type=MESH).start()

    for kind in KINDS:
        users = [d for d in range(N_DEV) if any(tuple(n for _, n, _ in sweep) == kind for sweep in PLAN[d])]
        uses = functools.reduce(jnp.logical_or, [me == d for d in users])

        @pl.when(uses)
        def _():
            first = 0
            for n in kind:
                for buf in bufs_of[kind]:
                    buf[pl.ds(first, pad), :] = jnp.zeros((pad, chan), F32)
                first += pad + n * blk

    for copy in w_copies:
        copy.wait()

    def halve(l, carry):
        wg_v[l, :, pl.ds(chan, chan)] = wg_v[l, :, pl.ds(chan, chan)] * BF16(0.5)
        wo_v[l] = wo_v[l] * BF16(0.5)
        return carry

    lax.fori_loop(0, n_layers, halve, 0)

    def compute(q, kind):
        bufs = bufs_of[kind]
        base, first = [], 0
        for n in kind:
            base += [first + pad + b * blk for b in range(n)]
            first += pad + n * blk
        count = len(base)
        lag = LAG if count > 4 else 1

        arrived = xbuf.at[q, pl.ds(0, count)]
        pltpu.make_async_copy(arrived, arrived, x_recv.at[q]).wait()
        for k in range(count):
            bufs[0][pl.ds(base[k], blk), :] = xbuf[q, k].astype(F32)
            skip_v[q, k] = jnp.zeros((blk, chan), F32)

        def gates(l, dil, par, k):
            lhs = jnp.concatenate([bufs[par][pl.ds(base[k], blk), :], bufs[par][pl.ds(base[k] - dil, blk), :]], axis=1).astype(BF16)
            return jnp.dot(lhs, wg_v[l], preferred_element_type=F32)

        def activate(l, pre):
            act = (jnp.tanh(pre[:, :chan]) * (1.0 + jnp.tanh(pre[:, chan:]))).astype(BF16)
            return jnp.dot(act, wo_v[l], preferred_element_type=F32)

        def update(par, k, mixed):
            bufs[1 - par][pl.ds(base[k], blk), :] = bufs[par][pl.ds(base[k], blk), :] + mixed[:, :chan]
            skip_v[q, k] = skip_v[q, k] + mixed[:, chan:]

        def cycle(r, carry):
            steps = [(c, k) for c in range(n_cyc) for k in range(count)]
            pre, mixed = {}, {}
            for t in range(len(steps) + 2 * lag):
                if t < len(steps):
                    c, k = steps[t]
                    pre[t] = gates(r * n_cyc + c, 2**c, c % 2, k)
                if 0 <= t - lag < len(steps):
                    c, k = steps[t - lag]
                    mixed[t - lag] = activate(r * n_cyc + c, pre.pop(t - lag))
                if 0 <= t - 2 * lag:
                    c, k = steps[t - 2 * lag]
                    update(c % 2, k, mixed.pop(t - 2 * lag))
            return carry

        lax.fori_loop(0, n_layers // n_cyc, cycle, 0)
        for k in range(count):
            hout_v[q, k] = bufs[0][pl.ds(base[k], blk), :]

    def deliver(src, q):
        out = [(k, seq, b) for k, seq, b, counts in units(PLAN[src][q]) if counts]
        for k, seq, b in sorted(out, key=lambda u: ((src // 2) ^ (u[2] // 2) != 3, u)):
            for part, dst, recv in ((hout_v, h_out, h_recv), (skip_v, s_out, s_recv)):
                if b == src:
                    dst[seq] = part[q, k]
                else:
                    pltpu.make_async_remote_copy(
                        src_ref=part.at[q, k], dst_ref=dst.at[seq], send_sem=o_send, recv_sem=recv,
                        device_id=dev(b), device_id_type=MESH).start()

    def run(q, carry):
        for kind in KINDS:
            where = [(d, i) for d in range(N_DEV) for i, sweep in enumerate(PLAN[d]) if tuple(n for _, n, _ in sweep) == kind]
            hit = functools.reduce(jnp.logical_or, [jnp.logical_and(me == d, q == i) for d, i in where])

            @pl.when(hit)
            def _():
                compute(q, kind)

        for d in range(N_DEV):
            @on(d)
            def _():
                for i in range(len(PLAN[d])):
                    @pl.when(q == i)
                    def _():
                        deliver(d, i)
        return carry

    lax.fori_loop(0, N_SWEEP, run, 0)

    def drain(ref, sem, count):
        while count > 0:
            part = ref.at[pl.ds(0, min(count, n_seq))]
            pltpu.make_async_copy(part, part, sem).wait()
            count -= n_seq

    for d in range(N_DEV):
        @on(d)
        def _():
            drain(x_own, x_send, sum(target != d for _, _, target, _, _ in wanted[d]))
            results = [b for q in range(len(PLAN[d])) for _, _, b, counts in units(PLAN[d][q]) if counts]
            kept = results.count(d)
            drain(h_out, o_send, 2 * (len(results) - kept))
            drain(h_out, h_recv, n_seq - kept)
            drain(s_out, s_recv, n_seq - kept)


def to_hbm(h_vmem, s_vmem, h_hbm, s_hbm, sems):
    piece = h_vmem.shape[0] // PIECES
    copies = []
    for i in range(PIECES):
        rows = pl.ds(i * piece, piece)
        for j, (src, dst) in enumerate(((h_vmem, h_hbm), (s_vmem, s_hbm))):
            copies.append(pltpu.make_async_copy(src.at[rows], dst.at[rows], sems.at[j, i]))
    for copy in copies:
        copy.start()
    for copy in copies:
        copy.wait()


def solution(mesh):
    seq_spec = P("batch", SEQ_AXES, None)

    def local_stack(x_loc, w_f0, w_f1, w_g0, w_g1, w_res, w_skip):
        n_rep, n_cyc, chan = w_f0.shape[:3]
        n_layers = n_rep * n_cyc
        n_seq, blk, _ = x_loc.shape
        pad = 2 ** (n_cyc - 1)
        weights = [w.reshape(n_layers, chan, chan) for w in (w_f0, w_f1, w_g0, w_g1, w_res, w_skip)]
        any_spec = pl.BlockSpec(memory_space=pl.ANY)
        vmem_spec = pl.BlockSpec(memory_space=pltpu.VMEM)
        out = jax.ShapeDtypeStruct((n_seq, blk, chan), F32)
        vmem_out = pltpu.VMEM((n_seq, blk, chan), F32)
        state = [pltpu.VMEM((sum(pad + n * blk for n in kind), chan), F32) for kind in KINDS for _ in range(2)]
        landed = pl.pallas_call(
            functools.partial(kernel, n_layers, n_cyc, blk, pad),
            out_shape=(vmem_out, vmem_out),
            in_specs=[any_spec] * 7,
            out_specs=(vmem_spec, vmem_spec),
            scratch_shapes=[
                pltpu.VMEM((n_seq, blk, chan), BF16),
                pltpu.VMEM((N_SWEEP, 8, blk, chan), BF16),
                pltpu.VMEM((n_layers, 2 * chan, 2 * chan), BF16),
                pltpu.VMEM((n_layers, chan, 2 * chan), BF16),
                pltpu.VMEM((N_SWEEP, 8, blk, chan), F32),
                pltpu.VMEM((N_SWEEP, 8, blk, chan), F32),
                pltpu.SemaphoreType.DMA((6,)),
                pltpu.SemaphoreType.DMA,
                pltpu.SemaphoreType.DMA,
                pltpu.SemaphoreType.DMA((N_SWEEP,)),
                pltpu.SemaphoreType.DMA,
                pltpu.SemaphoreType.DMA,
                pltpu.SemaphoreType.DMA,
                *state,
            ],
            compiler_params=pltpu.CompilerParams(collective_id=0, has_side_effects=True, vmem_limit_bytes=44 * 2**20),
        )(*[pltpu.with_memory_space_constraint(v, pltpu.HBM) for v in (x_loc, *weights)])
        return pl.pallas_call(
            to_hbm,
            out_shape=(out, out),
            in_specs=[vmem_spec, vmem_spec],
            out_specs=(any_spec, any_spec),
            scratch_shapes=[pltpu.SemaphoreType.DMA((2, PIECES))],
            compiler_params=pltpu.CompilerParams(vmem_limit_bytes=2 * 2**20),
        )(*landed)

    return jax.shard_map(local_stack, mesh=mesh, in_specs=(seq_spec, P(), P(), P(), P(), P(), P()), out_specs=(seq_spec, seq_spec), check_vma=False)
```

profile of v0, /device:TPU:5, one launch (start us, length us, event | category | flops | bytes accessed | tf_op | source)
XLA Modules:
  0.0 58.4 jit_solution(5609594741022099466)
XLA Ops:
  0.6 55.6 %shard_map.86 = (f32[24,192,128]{2,1,0:T(8,128)S(1)}, f32[24,192,128]{2,1,0:T(8,128)S(1)}) custom-call(bf16[24,192,128]{2,1,0:T(8,128)(2,1)} %x_ref.1, bf16[20,128,128]{2,1,0:T(8,128)(2,1)} %bitcast.6, bf16[20,128,128]{2,1,0:T(8,128)(2,1)} %bitcast.7, bf16[20,128,128]{2,1,0:T(8,128)(2,1)} %bitcast.8, bf16[20,128,128]{2,1,0:T(8,128)(2,1)} %bitcast.9, ...), custom_call_target="tpu_custom_call" | custom-call | tf_op jit(solution)/shard_map/pallas_call | solution.py:268
  56.2 2.2 %shard_map.87 = (f32[24,192,128]{2,1,0:T(8,128)}, f32[24,192,128]{2,1,0:T(8,128)}) custom-call(f32[24,192,128]{2,1,0:T(8,128)S(1)} %get-tuple-element.4.h_vmem, f32[24,192,128]{2,1,0:T(8,128)S(1)} %get-tuple-element.5.s_vmem), custom_call_target="tpu_custom_call" | custom-call | tf_op jit(solution)/shard_map/pallas_call | solution.py:291
where the time goes:
time: 58.5 us; the launch traced here: 58.4 us
  Pallas kernels  57.8 us (99%)
  between operations  0.64 us (1%)
    pallas_call x1, Pallas kernels, local_stack(): pl.pallas_call(functools.partial(kernel, n_layers, n_cyc, blk, pad), out_...  55.6 us
    pallas_call x1, Pallas kernels, local_stack(): pl.pallas_call(to_hbm, out_shape=(out, out), in_specs=[vmem_spec, vmem_sp...  2.24 us

commit v1 on v0

--- a/solution.py
+++ b/solution.py
@@ -151,44 +151,46 @@
             base += [first + pad + b * blk for b in range(n)]
             first += pad + n * blk
         count = len(base)
+        everywhere = [units(sweep) for sweeps in PLAN for sweep in sweeps if tuple(n for _, n, _ in sweep) == kind]
+        unused = [k for k in range(count) if not any(listed[k][3] for listed in everywhere)]
         lag = LAG if count > 4 else 1
 
         arrived = xbuf.at[q, pl.ds(0, count)]
         pltpu.make_async_copy(arrived, arrived, x_recv.at[q]).wait()
-        for k in range(count):
+
+        def begin(k):
             bufs[0][pl.ds(base[k], blk), :] = xbuf[q, k].astype(F32)
-            skip_v[q, k] = jnp.zeros((blk, chan), F32)
-
-        def gates(l, dil, par, k):
-            lhs = jnp.concatenate([bufs[par][pl.ds(base[k], blk), :], bufs[par][pl.ds(base[k] - dil, blk), :]], axis=1).astype(BF16)
+
+        def gates(l, k):
+            here, dil = bufs[l % 2], 2 ** (l % n_cyc)
+            lhs = jnp.concatenate([here[pl.ds(base[k], blk), :], here[pl.ds(base[k] - dil, blk), :]], axis=1).astype(BF16)
             return jnp.dot(lhs, wg_v[l], preferred_element_type=F32)
 
         def activate(l, pre):
             act = (jnp.tanh(pre[:, :chan]) * (1.0 + jnp.tanh(pre[:, chan:]))).astype(BF16)
             return jnp.dot(act, wo_v[l], preferred_element_type=F32)
 
-        def update(par, k, mixed):
-            bufs[1 - par][pl.ds(base[k], blk), :] = bufs[par][pl.ds(base[k], blk), :] + mixed[:, :chan]
-            skip_v[q, k] = skip_v[q, k] + mixed[:, chan:]
-
-        def cycle(r, carry):
-            steps = [(c, k) for c in range(n_cyc) for k in range(count)]
-            pre, mixed = {}, {}
-            for t in range(len(steps) + 2 * lag):
-                if t < len(steps):
-                    c, k = steps[t]
-                    pre[t] = gates(r * n_cyc + c, 2**c, c % 2, k)
-                if 0 <= t - lag < len(steps):
-                    c, k = steps[t - lag]
-                    mixed[t - lag] = activate(r * n_cyc + c, pre.pop(t - lag))
-                if 0 <= t - 2 * lag:
-                    c, k = steps[t - 2 * lag]
-                    update(c % 2, k, mixed.pop(t - 2 * lag))
-            return carry
-
-        lax.fori_loop(0, n_layers // n_cyc, cycle, 0)
-        for k in range(count):
-            hout_v[q, k] = bufs[0][pl.ds(base[k], blk), :]
+        def update(l, k, mixed):
+            new = bufs[l % 2][pl.ds(base[k], blk), :] + mixed[:, :chan]
+            if l == n_layers - 1:
+                hout_v[q, k] = new
+            else:
+                bufs[1 - l % 2][pl.ds(base[k], blk), :] = new
+            skip_v[q, k] = mixed[:, chan:] if l == 0 else skip_v[q, k] + mixed[:, chan:]
+
+        steps = [(l, k) for l in range(n_layers) for k in range(count) if l < n_layers - 1 or k not in unused]
+        pre, mixed = {}, {}
+        for t in range(len(steps) + 2 * lag):
+            if t < len(steps):
+                if t == 0:
+                    begin(0)
+                if t + 1 < count:
+                    begin(t + 1)
+                pre[t] = gates(*steps[t])
+            if 0 <= t - lag < len(steps):
+                mixed[t - lag] = activate(steps[t - lag][0], pre.pop(t - lag))
+            if 0 <= t - 2 * lag:
+                update(*steps[t - 2 * lag], mixed.pop(t - 2 * lag))
 
     def deliver(src, q):
         out = [(k, seq, b) for k, seq, b, counts in units(PLAN[src][q]) if counts]

time: 58.5 us -> 58.5 us (level); the launches traced: 58.4 us -> 57.8 us
  Pallas kernels: 57.8 us -> 57.2 us
    pallas_call x1, Pallas kernels: 55.6 us -> 54.9 us  [local_stack(): pl.pallas_call(functools.partial(kernel, n_layers, n_cyc, blk, pad), out_...]
where the time goes in v1:
time: 58.5 us; the launch traced here: 57.8 us
  Pallas kernels  57.2 us (98%)
  between operations  0.64 us (1%)
    pallas_call x1, Pallas kernels, local_stack(): pl.pallas_call(functools.partial(kernel, n_layers, n_cyc, blk, pad), out_...  54.9 us
    pallas_call x1, Pallas kernels, local_stack(): pl.pallas_call(to_hbm, out_shape=(out, out), in_specs=[vmem_spec, vmem_sp...  2.24 us

profile of v1, /device:TPU:5, one launch (start us, length us, event | category | flops | bytes accessed | tf_op | source)
XLA Modules:
  0.0 57.8 jit_solution(15839586200729993029)
XLA Ops:
  0.6 54.9 %shard_map.86 = (f32[24,192,128]{2,1,0:T(8,128)S(1)}, f32[24,192,128]{2,1,0:T(8,128)S(1)}) custom-call(bf16[24,192,128]{2,1,0:T(8,128)(2,1)} %x_ref.1, bf16[20,128,128]{2,1,0:T(8,128)(2,1)} %bitcast.6, bf16[20,128,128]{2,1,0:T(8,128)(2,1)} %bitcast.7, bf16[20,128,128]{2,1,0:T(8,128)(2,1)} %bitcast.8, bf16[20,128,128]{2,1,0:T(8,128)(2,1)} %bitcast.9, ...), custom_call_target="tpu_custom_call" | custom-call | tf_op jit(solution)/shard_map/pallas_call | solution.py:270
  55.6 2.2 %shard_map.87 = (f32[24,192,128]{2,1,0:T(8,128)}, f32[24,192,128]{2,1,0:T(8,128)}) custom-call(f32[24,192,128]{2,1,0:T(8,128)S(1)} %get-tuple-element.4.h_vmem, f32[24,192,128]{2,1,0:T(8,128)S(1)} %get-tuple-element.5.s_vmem), custom_call_target="tpu_custom_call" | custom-call | tf_op jit(solution)/shard_map/pallas_call | solution.py:293

commit v2 on v0

--- a/solution.py
+++ b/solution.py
@@ -12,57 +12,63 @@
 N_DEV = 8
 PIECES = 4
 LAG = 2
+UNROLLED = ((8,), (4, 4))
 F32 = jnp.float32
 BF16 = jnp.bfloat16
 
 PLAN = (
     (
-        ((8, 4, (0, 1, 2, 3)), (9, 4, (0, 1, 2, 3)),),
-        ((10, 4, (0, 1, 2, 3)), (11, 4, (0, 1, 2, 3)),),
-        ((0, 2, (0, 1)), (1, 2, (0, 1)), (2, 2, (0, 1)), (3, 2, (0, 1)),),
-        ((4, 2, (0, 1)), (5, 2, (0, 1)), (6, 2, (0, 1)), (7, 2, (0, 1)),),
-    ),
-    (
-        ((12, 4, (0, 1, 2, 3)), (13, 4, (0, 1, 2, 3)),),
-        ((14, 4, (0, 1, 2, 3)), (15, 4, (0, 1, 2, 3)),),
-        ((16, 2, (0, 1)), (17, 2, (0, 1)), (18, 2, (0, 1)), (19, 2, (0, 1)),),
-        ((20, 2, (0, 1)), (21, 2, (0, 1)), (22, 2, (0, 1)), (23, 2, (0, 1)),),
-    ),
-    (
-        ((0, 8, (2, 3, 4, 5, 6, 7)),),
+        ((19, 2, (0, 1)), (4, 2, (0, 1)), (6, 2, (0, 1)), (21, 2, (0, 1)),),
+        ((14, 6, (0, 1, 2, 3, 4, 5)),),
+        ((23, 6, (0, 1, 4, 5)),),
+        ((22, 4, (0, 1, 2, 3)), (16, 4, (0, 1, 2, 3)),),
+        ((12, 2, (0, 1)), (3, 2, (0, 1)), (13, 2, (0, 1)), (11, 2, (0, 1)),),
+    ),
+    (
+        ((15, 8, (0, 1, 4, 5, 6, 7)),),
+        ((18, 8, (0, 1, 4, 5, 6, 7)),),
+        ((20, 2, (0, 1)), (1, 2, (0, 1)), (8, 2, (0, 1)), (7, 2, (0, 1)),),
+        ((10, 2, (0, 1)), (2, 2, (0, 1)), (0, 2, (0, 1)), (9, 2, (0, 1)),),
+    ),
+    (
+        ((20, 4, (2, 3)), (10, 4, (2, 3)),),
+        ((21, 8, (2, 3, 6, 7)),),
+        ((23, 8, (2, 3, 6, 7)),),
+        ((18, 4, (2, 3)), (9, 4, (2, 3)),),
+    ),
+    (
+        ((13, 8, (2, 3, 4, 5, 6, 7)),),
+        ((12, 8, (2, 3, 6, 7)),),
+        ((5, 8, (0, 1, 2, 3, 4, 5, 6, 7)),),
+        ((0, 4, (2, 3)), (17, 4, (2, 3)),),
+        ((15, 4, (2, 3)), (3, 4, (2, 3)),),
+    ),
+    (
+        ((22, 8, (4, 5, 6, 7)),),
+        ((20, 8, (4, 5, 6, 7)),),
+        ((3, 8, (4, 5, 6, 7)),),
+        ((16, 8, (4, 5, 6, 7)),),
+        ((12, 6, (4, 5)),),
+    ),
+    (
+        ((10, 8, (4, 5, 6, 7)),),
+        ((9, 8, (4, 5, 6, 7)),),
+        ((17, 8, (0, 1, 4, 5, 6, 7)),),
+        ((0, 8, (4, 5, 6, 7)),),
+        ((21, 6, (4, 5)),),
+    ),
+    (
+        ((8, 8, (2, 3, 4, 5, 6, 7)),),
+        ((7, 8, (2, 3, 4, 5, 6, 7)),),
+        ((2, 8, (2, 3, 4, 5, 6, 7)),),
+        ((6, 8, (2, 3, 4, 5, 6, 7)),),
+    ),
+    (
+        ((11, 8, (2, 3, 4, 5, 6, 7)),),
+        ((4, 8, (2, 3, 4, 5, 6, 7)),),
         ((1, 8, (2, 3, 4, 5, 6, 7)),),
-        ((2, 8, (2, 3, 4, 5, 6, 7)),),
-        ((3, 8, (2, 3, 4, 5, 6, 7)),),
-    ),
-    (
-        ((4, 8, (2, 3, 4, 5, 6, 7)),),
-        ((5, 8, (2, 3, 4, 5, 6, 7)),),
-        ((6, 8, (2, 3, 4, 5, 6, 7)),),
-        ((7, 8, (2, 3, 4, 5, 6, 7)),),
-    ),
-    (
-        ((8, 8, (4, 5, 6, 7)),),
-        ((9, 8, (4, 5, 6, 7)),),
-        ((10, 8, (4, 5, 6, 7)),),
-        ((11, 8, (4, 5, 6, 7)),),
-    ),
-    (
-        ((12, 8, (4, 5, 6, 7)),),
-        ((13, 8, (4, 5, 6, 7)),),
-        ((14, 8, (4, 5, 6, 7)),),
-        ((15, 8, (4, 5, 6, 7)),),
-    ),
-    (
-        ((16, 8, (2, 3, 4, 5, 6, 7)),),
-        ((17, 8, (2, 3, 4, 5, 6, 7)),),
-        ((18, 8, (2, 3, 4, 5, 6, 7)),),
         ((19, 8, (2, 3, 4, 5, 6, 7)),),
-    ),
-    (
-        ((20, 8, (2, 3, 4, 5, 6, 7)),),
-        ((21, 8, (2, 3, 4, 5, 6, 7)),),
-        ((22, 8, (2, 3, 4, 5, 6, 7)),),
-        ((23, 8, (2, 3, 4, 5, 6, 7)),),
+        ((14, 8, (6, 7)),),
     ),
 )
 N_SWEEP = max(len(sweeps) for sweeps in PLAN)
@@ -110,7 +116,7 @@
     for target, sweeps in enumerate(PLAN):
         for q, sweep in enumerate(sweeps):
             for k, seq, b, _ in units(sweep):
-                wanted[b].append((q, (target // 2) ^ (b // 2) != 3, target, k, seq))
+                wanted[b].append((q, ((target // 2) ^ (b // 2) != 3, target % 2 == 0), target, k, seq))
     for src in range(N_DEV):
         @on(src)
         def _():
@@ -151,48 +157,67 @@
             base += [first + pad + b * blk for b in range(n)]
             first += pad + n * blk
         count = len(base)
+        everywhere = [units(sweep) for sweeps in PLAN for sweep in sweeps if tuple(n for _, n, _ in sweep) == kind]
+        unused = [k for k in range(count) if not any(listed[k][3] for listed in everywhere)]
         lag = LAG if count > 4 else 1
 
         arrived = xbuf.at[q, pl.ds(0, count)]
         pltpu.make_async_copy(arrived, arrived, x_recv.at[q]).wait()
-        for k in range(count):
+
+        def begin(k):
             bufs[0][pl.ds(base[k], blk), :] = xbuf[q, k].astype(F32)
-            skip_v[q, k] = jnp.zeros((blk, chan), F32)
-
-        def gates(l, dil, par, k):
-            lhs = jnp.concatenate([bufs[par][pl.ds(base[k], blk), :], bufs[par][pl.ds(base[k] - dil, blk), :]], axis=1).astype(BF16)
+
+        def gates(l, c, k):
+            here = bufs[c % 2]
+            lhs = jnp.concatenate([here[pl.ds(base[k], blk), :], here[pl.ds(base[k] - 2**c, blk), :]], axis=1).astype(BF16)
             return jnp.dot(lhs, wg_v[l], preferred_element_type=F32)
 
         def activate(l, pre):
             act = (jnp.tanh(pre[:, :chan]) * (1.0 + jnp.tanh(pre[:, chan:]))).astype(BF16)
             return jnp.dot(act, wo_v[l], preferred_element_type=F32)
 
-        def update(par, k, mixed):
-            bufs[1 - par][pl.ds(base[k], blk), :] = bufs[par][pl.ds(base[k], blk), :] + mixed[:, :chan]
-            skip_v[q, k] = skip_v[q, k] + mixed[:, chan:]
-
-        def cycle(r, carry):
-            steps = [(c, k) for c in range(n_cyc) for k in range(count)]
+        def update(c, k, mixed, first, last):
+            new = bufs[c % 2][pl.ds(base[k], blk), :] + mixed[:, :chan]
+            if last:
+                hout_v[q, k] = new
+            else:
+                bufs[1 - c % 2][pl.ds(base[k], blk), :] = new
+            skip_v[q, k] = mixed[:, chan:] if first else skip_v[q, k] + mixed[:, chan:]
+
+        def layers(steps, layer_of, whole):
             pre, mixed = {}, {}
             for t in range(len(steps) + 2 * lag):
                 if t < len(steps):
+                    if whole and t == 0:
+                        begin(0)
+                    if whole and t + 1 < count:
+                        begin(t + 1)
                     c, k = steps[t]
-                    pre[t] = gates(r * n_cyc + c, 2**c, c % 2, k)
+                    pre[t] = gates(layer_of(c), c % n_cyc, k)
                 if 0 <= t - lag < len(steps):
-                    c, k = steps[t - lag]
-                    mixed[t - lag] = activate(r * n_cyc + c, pre.pop(t - lag))
+                    mixed[t - lag] = activate(layer_of(steps[t - lag][0]), pre.pop(t - lag))
                 if 0 <= t - 2 * lag:
                     c, k = steps[t - 2 * lag]
-                    update(c % 2, k, mixed.pop(t - 2 * lag))
-            return carry
-
-        lax.fori_loop(0, n_layers // n_cyc, cycle, 0)
-        for k in range(count):
-            hout_v[q, k] = bufs[0][pl.ds(base[k], blk), :]
+                    update(c % n_cyc, k, mixed.pop(t - 2 * lag), whole and c == 0, whole and c == n_layers - 1)
+
+        if kind in UNROLLED:
+            layers([(c, k) for c in range(n_layers) for k in range(count) if c < n_layers - 1 or k not in unused], lambda c: c, True)
+        else:
+            for k in range(count):
+                begin(k)
+                skip_v[q, k] = jnp.zeros((blk, chan), F32)
+
+            def cycle(r, carry):
+                layers([(c, k) for c in range(n_cyc) for k in range(count)], lambda c: r * n_cyc + c, False)
+                return carry
+
+            lax.fori_loop(0, n_layers // n_cyc, cycle, 0)
+            for k in range(count):
+                hout_v[q, k] = bufs[0][pl.ds(base[k], blk), :]
 
     def deliver(src, q):
         out = [(k, seq, b) for k, seq, b, counts in units(PLAN[src][q]) if counts]
-        for k, seq, b in sorted(out, key=lambda u: ((src // 2) ^ (u[2] // 2) != 3, u)):
+        for k, seq, b in sorted(out, key=lambda u: ((src // 2) ^ (u[2] // 2) != 3, u[2] % 2 == 0, u)):
             for part, dst, recv in ((hout_v, h_out, h_recv), (skip_v, s_out, s_recv)):
                 if b == src:
                     dst[seq] = part[q, k]

time: 58.5 us -> 56.4 us (0.964)
  Pallas kernels: 57.8 us -> 55.6 us
    pallas_call x1, Pallas kernels: 55.6 us -> 53.4 us  [local_stack(): pl.pallas_call(functools.partial(kernel, n_layers, n_cyc, blk, pad), out_...]
where the time goes in v2:
time: 56.4 us; the launch traced here: 56.3 us
  Pallas kernels  55.6 us (99%)
  between operations  0.64 us (1%)
    pallas_call x1, Pallas kernels, local_stack(): pl.pallas_call(functools.partial(kernel, n_layers, n_cyc, blk, pad), out_...  53.4 us
    pallas_call x1, Pallas kernels, local_stack(): pl.pallas_call(to_hbm, out_shape=(out, out), in_specs=[vmem_spec, vmem_sp...  2.24 us

profile of v2, /device:TPU:5, one launch (start us, length us, event | category | flops | bytes accessed | tf_op | source)
XLA Modules:
  0.0 56.3 jit_solution(18433175758375988141)
XLA Ops:
  0.6 53.4 %shard_map.86 = (f32[24,192,128]{2,1,0:T(8,128)S(1)}, f32[24,192,128]{2,1,0:T(8,128)S(1)}) custom-call(bf16[24,192,128]{2,1,0:T(8,128)(2,1)} %x_ref.1, bf16[20,128,128]{2,1,0:T(8,128)(2,1)} %bitcast.6, bf16[20,128,128]{2,1,0:T(8,128)(2,1)} %bitcast.7, bf16[20,128,128]{2,1,0:T(8,128)(2,1)} %bitcast.8, bf16[20,128,128]{2,1,0:T(8,128)(2,1)} %bitcast.9, ...), custom_call_target="tpu_custom_call" | custom-call | tf_op jit(solution)/shard_map/pallas_call | solution.py:293
  54.0 2.2 %shard_map.87 = (f32[24,192,128]{2,1,0:T(8,128)}, f32[24,192,128]{2,1,0:T(8,128)}) custom-call(f32[24,192,128]{2,1,0:T(8,128)S(1)} %get-tuple-element.4.h_vmem, f32[24,192,128]{2,1,0:T(8,128)S(1)} %get-tuple-element.5.s_vmem), custom_call_target="tpu_custom_call" | custom-call | tf_op jit(solution)/shard_map/pallas_call | solution.py:316

commit v3 on v2

--- a/solution.py
+++ b/solution.py
@@ -12,7 +12,7 @@
 N_DEV = 8
 PIECES = 4
 LAG = 2
-UNROLLED = ((8,), (4, 4))
+UNROLLED = ((8,), (6,), (4, 4))
 F32 = jnp.float32
 BF16 = jnp.bfloat16
 
@@ -91,6 +91,11 @@
 
     def on(index):
         return pl.when(me == index)
+
+    barrier = pltpu.get_barrier_semaphore()
+    for step in range(1, N_DEV):
+        other = lax.rem(me + step, N_DEV)
+        pl.semaphore_signal(barrier, inc=1, device_id={"seq_hi": other // 4, "seq": lax.rem(other, 4)}, device_id_type=MESH)
 
     own = pltpu.make_async_copy(x_ref, x_own, own_sem)
     own.start()
@@ -105,10 +110,6 @@
     for copy in w_copies:
         copy.start()
 
-    barrier = pltpu.get_barrier_semaphore()
-    for step in range(1, N_DEV):
-        other = lax.rem(me + step, N_DEV)
-        pl.semaphore_signal(barrier, inc=1, device_id={"seq_hi": other // 4, "seq": lax.rem(other, 4)}, device_id_type=MESH)
     pl.semaphore_wait(barrier, N_DEV - 1)
     own.wait()
 

time: 56.4 us -> 56 us (level)
  no operation moved by 1% of the time
where the time goes in v3:
time: 56 us; the launch traced here: 55.9 us
  Pallas kernels  55.3 us (99%)
  between operations  0.64 us (1%)
    pallas_call x1, Pallas kernels, local_stack(): pl.pallas_call(functools.partial(kernel, n_layers, n_cyc, blk, pad), out_...  53 us
    pallas_call x1, Pallas kernels, local_stack(): pl.pallas_call(to_hbm, out_shape=(out, out), in_specs=[vmem_spec, vmem_sp...  2.24 us

profile of v3, /device:TPU:5, one launch (start us, length us, event | category | flops | bytes accessed | tf_op | source)
XLA Modules:
  0.0 55.9 jit_solution(16522171957772925060)
XLA Ops:
  0.6 53.0 %shard_map.86 = (f32[24,192,128]{2,1,0:T(8,128)S(1)}, f32[24,192,128]{2,1,0:T(8,128)S(1)}) custom-call(bf16[24,192,128]{2,1,0:T(8,128)(2,1)} %x_ref.1, bf16[20,128,128]{2,1,0:T(8,128)(2,1)} %bitcast.6, bf16[20,128,128]{2,1,0:T(8,128)(2,1)} %bitcast.7, bf16[20,128,128]{2,1,0:T(8,128)(2,1)} %bitcast.8, bf16[20,128,128]{2,1,0:T(8,128)(2,1)} %bitcast.9, ...), custom_call_target="tpu_custom_call" | custom-call | tf_op jit(solution)/shard_map/pallas_call | solution.py:294
  53.6 2.2 %shard_map.87 = (f32[24,192,128]{2,1,0:T(8,128)}, f32[24,192,128]{2,1,0:T(8,128)}) custom-call(f32[24,192,128]{2,1,0:T(8,128)S(1)} %get-tuple-element.4.h_vmem, f32[24,192,128]{2,1,0:T(8,128)S(1)} %get-tuple-element.5.s_vmem), custom_call_target="tpu_custom_call" | custom-call | tf_op jit(solution)/shard_map/pallas_call | solution.py:317

commit v4 on v3

--- a/solution.py
+++ b/solution.py
@@ -117,7 +117,7 @@
     for target, sweeps in enumerate(PLAN):
         for q, sweep in enumerate(sweeps):
             for k, seq, b, _ in units(sweep):
-                wanted[b].append((q, ((target // 2) ^ (b // 2) != 3, target % 2 == 0), target, k, seq))
+                wanted[b].append((q, ((target // 2) ^ (b // 2) != 3, (target % 2 == 0) != (target // 2 == 2)), target, k, seq))
     for src in range(N_DEV):
         @on(src)
         def _():

time: 56 us -> 55.8 us (level)
  no operation moved by 1% of the time
where the time goes in v4:
time: 55.8 us; the launch traced here: 55.7 us
  Pallas kernels  55 us (99%)
  between operations  0.64 us (1%)
    pallas_call x1, Pallas kernels, local_stack(): pl.pallas_call(functools.partial(kernel, n_layers, n_cyc, blk, pad), out_...  52.8 us
    pallas_call x1, Pallas kernels, local_stack(): pl.pallas_call(to_hbm, out_shape=(out, out), in_specs=[vmem_spec, vmem_sp...  2.24 us

profile of v4, /device:TPU:5, one launch (start us, length us, event | category | flops | bytes accessed | tf_op | source)
XLA Modules:
  0.0 55.7 jit_solution(4600680969226043149)
XLA Ops:
  0.6 52.8 %shard_map.86 = (f32[24,192,128]{2,1,0:T(8,128)S(1)}, f32[24,192,128]{2,1,0:T(8,128)S(1)}) custom-call(bf16[24,192,128]{2,1,0:T(8,128)(2,1)} %x_ref.1, bf16[20,128,128]{2,1,0:T(8,128)(2,1)} %bitcast.6, bf16[20,128,128]{2,1,0:T(8,128)(2,1)} %bitcast.7, bf16[20,128,128]{2,1,0:T(8,128)(2,1)} %bitcast.8, bf16[20,128,128]{2,1,0:T(8,128)(2,1)} %bitcast.9, ...), custom_call_target="tpu_custom_call" | custom-call | tf_op jit(solution)/shard_map/pallas_call | solution.py:294
  53.4 2.2 %shard_map.87 = (f32[24,192,128]{2,1,0:T(8,128)}, f32[24,192,128]{2,1,0:T(8,128)}) custom-call(f32[24,192,128]{2,1,0:T(8,128)S(1)} %get-tuple-element.4.h_vmem, f32[24,192,128]{2,1,0:T(8,128)S(1)} %get-tuple-element.5.s_vmem), custom_call_target="tpu_custom_call" | custom-call | tf_op jit(solution)/shard_map/pallas_call | solution.py:317

commit v5 on v4

--- a/solution.py
+++ b/solution.py
@@ -10,7 +10,7 @@
 MESH = pl.DeviceIdType.MESH
 SEQ_AXES = ("seq_hi", "seq")
 N_DEV = 8
-PIECES = 4
+PIECES = 8
 LAG = 2
 UNROLLED = ((8,), (6,), (4, 4))
 F32 = jnp.float32

time: 55.8 us -> 55.8 us (level)
  no operation moved by 1% of the time
where the time goes in v5:
time: 55.8 us; the launch traced here: 55.7 us
  Pallas kernels  55.1 us (99%)
  between operations  0.64 us (1%)
    pallas_call x1, Pallas kernels, local_stack(): pl.pallas_call(functools.partial(kernel, n_layers, n_cyc, blk, pad), out_...  52.8 us
    pallas_call x1, Pallas kernels, local_stack(): pl.pallas_call(to_hbm, out_shape=(out, out), in_specs=[vmem_spec, vmem_sp...  2.31 us

profile of v5, /device:TPU:5, one launch (start us, length us, event | category | flops | bytes accessed | tf_op | source)
XLA Modules:
  0.0 55.7 jit_solution(17618403615943700193)
XLA Ops:
  0.6 52.8 %shard_map.86 = (f32[24,192,128]{2,1,0:T(8,128)S(1)}, f32[24,192,128]{2,1,0:T(8,128)S(1)}) custom-call(bf16[24,192,128]{2,1,0:T(8,128)(2,1)} %x_ref.1, bf16[20,128,128]{2,1,0:T(8,128)(2,1)} %bitcast.6, bf16[20,128,128]{2,1,0:T(8,128)(2,1)} %bitcast.7, bf16[20,128,128]{2,1,0:T(8,128)(2,1)} %bitcast.8, bf16[20,128,128]{2,1,0:T(8,128)(2,1)} %bitcast.9, ...), custom_call_target="tpu_custom_call" | custom-call | tf_op jit(solution)/shard_map/pallas_call | solution.py:294
  53.4 2.3 %shard_map.87 = (f32[24,192,128]{2,1,0:T(8,128)}, f32[24,192,128]{2,1,0:T(8,128)}) custom-call(f32[24,192,128]{2,1,0:T(8,128)S(1)} %get-tuple-element.4.h_vmem, f32[24,192,128]{2,1,0:T(8,128)S(1)} %get-tuple-element.5.s_vmem), custom_call_target="tpu_custom_call" | custom-call | tf_op jit(solution)/shard_map/pallas_call | solution.py:317
